TPU v7x, 32 devices: a whole 2x2x4 slice. The times are simulated.
32 devices in a mesh: gz: 8 (over z, y), gy: 4 (over x, core).
Axes of the slice: x: 2, y: 2, z: 4, core: 2. Of those that a mesh axis runs over, the one named last changes fastest.
Arguments:
- charge: float32 [393216], P(('gz', 'gy')), may hold values from -4 to 4
- fractions: float32 [3, 393216], P(None, ('gz', 'gy')), may hold values from 0 to 1
- cell_base: int32 [3, 393216], P(None, ('gz', 'gy')), may hold values from 0 to 255, as said below
- live_blocks: int32 [8, 4], P('gz'), may hold values from 12 to 96, as said below
- send_blocks: int32 [8, 4], P('gz'), may hold values from 0 to 36, as said below
- moduli: float32 [3, 256], replicated, may hold values from 0.5 to 2
- screening: float32 [1], replicated, may hold values from 8 to 16
Outputs:
- forces: float32 [3, 393216], P(None, ('gz', 'gy'))
Inputs may be any that keep to these rules, and one draw needn't show every extreme that they name: `cell_base`: row 0 lies in 0 to 31, row 1 in 0 to 63, row 2 in 0 to 255. `live_blocks`: a domain's live blocks are its first ones; in every row of the table some domain has 96 live blocks. send_blocks is at most the domain's live blocks; live_blocks minus send_blocks plus send_blocks of the domain before it along gy (cyclically) is at most 96; in every row some domain sends 36.
All inputs are finite; a program needn't handle non-finite values.
Results may differ from a plain program's by a relative error of at most 0.00023.
Values sent between devices are 32-bit elements; how exact they have to be, the bound alone decides.
A program may use at most 128 MiB of HBM per device.

v0:
```python
import functools

import jax
import jax.numpy as jnp
import numpy as np
from jax import lax
from jax.experimental import pallas as pl
from jax.experimental.pallas import tpu as pltpu
from jax.sharding import PartitionSpec as P

BLOCK = 128
SEND_MAX = 36
GROUP = 256
PAIR = 2
LAYER = 2
STEP = 7
WINDOW = 24
CHUNKS = 4
DEAD = 1 << 30

high = lax.Precision.HIGH
coulomb = 2.0


def shifted(x, axis, by):
    peers = lax.axis_size(axis)
    return lax.ppermute(x, axis, [(i, (i + by) % peers) for i in range(peers)])


def round_up(value, step):
    return -(-value // step) * step


def spline_weights(t):
    remain = 1.0 - t
    square = t * t
    cubed = square * t
    weights = [
        remain * remain * remain * (1.0 / 6.0),
        (3.0 * cubed - 6.0 * square + 4.0) * (1.0 / 6.0),
        (-3.0 * cubed + 3.0 * square + 3.0 * t + 1.0) * (1.0 / 6.0),
        cubed * (1.0 / 6.0),
    ]
    slopes = [
        -0.5 * remain * remain,
        1.5 * square - 2.0 * t,
        -1.5 * square + t + 0.5,
        0.5 * square,
    ]
    return weights, slopes


def stencil(base, weights, span):
    offset = lax.broadcasted_iota(jnp.int32, (span, base.shape[1]), 0) - base
    table = jnp.where(offset == 0, weights[0], 0.0)
    for k in range(1, 4):
        table = jnp.where(offset == k, weights[k], table)
    return table


def split(value):
    top = value.astype(jnp.bfloat16)
    rest = (value - top.astype(jnp.float32)).astype(jnp.bfloat16)
    return top, rest


def encode(cells, bits_y, bits_x):
    layer = cells[0] >> LAYER
    flip = (layer & 1) * ((1 << bits_y) - 1)
    inner = cells[0] & ((1 << LAYER) - 1)
    key = (layer << bits_y) | (cells[1] ^ flip)
    return (((key << LAYER) | inner) << bits_x) | cells[2]


def decode(key, bits_y, bits_x):
    inner = (key >> bits_x) & ((1 << LAYER) - 1)
    y = (key >> (bits_x + LAYER)) & ((1 << bits_y) - 1)
    layer = key >> (bits_x + LAYER + bits_y)
    y = y ^ ((layer & 1) * ((1 << bits_y) - 1))
    return (layer << LAYER) | inner, y, key & ((1 << bits_x) - 1)


def wrapped_stencil(places, base, weights, grid):
    top_table = rest_table = jnp.zeros(places.shape, jnp.bfloat16)
    for k in range(4):
        at = base + k
        at = jnp.where(at >= grid, at - grid, at).astype(jnp.float32).astype(jnp.bfloat16)
        hit = places == at
        top, rest = split(weights[k])
        top_table = jnp.where(hit, top, top_table)
        rest_table = jnp.where(hit, rest, rest_table)
    return top_table, rest_table


def fill_places(places):
    places[...] = (
        lax.broadcasted_iota(jnp.int32, places.shape, 0).astype(jnp.float32).astype(jnp.bfloat16)
    )


def over_windows(bounds, group, visit):
    low_z, high_z, low_y, high_y = (bounds[i, group] for i in range(4))
    start = (low_y // 8) * 8
    steps = (high_z + 3 - low_z) // STEP + 1
    strips = (high_y + 3 - start) // WINDOW + 1
    visit(low_z, start)

    def rest():
        @pl.loop(1, steps * strips)
        def _(at):
            visit(low_z + lax.rem(at, steps) * STEP, start + lax.div(at, steps) * WINDOW)

    return rest


def over_groups(atoms, prepare):
    @pl.loop(0, (atoms + PAIR * GROUP - 1) // (PAIR * GROUP))
    def _(turn):
        later = [prepare(turn * PAIR + i, i) for i in range(PAIR)]
        for rest in later:
            rest()


def spread_kernel(
    rows, grid, bits, count, bounds, key, charge, fz, fy, fx, tile, places, table_z, factor_x,
):
    tile[...] = jnp.zeros_like(tile)
    fill_places(places)
    atoms = count[0]

    def prepare(group, lane):
        at = pl.ds(pl.multiple_of(group * GROUP, GROUP), GROUP)
        place = group * GROUP + lax.broadcasted_iota(jnp.int32, (1, GROUP), 1)
        value = jnp.where(place < atoms, charge[0:1, at], 0.0)
        cell_z, cell_y, cell_x = decode(key[0:1, at], *bits)
        weight_z, _ = spline_weights(fz[0:1, at])
        weight_y, _ = spline_weights(fy[0:1, at])
        weight_x, _ = spline_weights(fx[0:1, at])
        weight_x = [value * w for w in weight_x]
        top, rest = wrapped_stencil(places[...], cell_x, weight_x, grid)
        factor_x[lane, :, :GROUP] = top
        factor_x[lane, :, GROUP:] = rest

        def visit(first, start):
            table_z[lane] = stencil(cell_z - first, weight_z, table_z.shape[1])
            table_y = stencil(cell_y - start, weight_y, WINDOW)
            part = jnp.concatenate([table_z[lane, j : j + 1, :] * table_y for j in range(STEP)], 0)
            top, rest = split(part)
            across = (((1,), (1,)), ((), ()))
            values = lax.dot_general(
                jnp.concatenate([top, rest], 0), factor_x[lane, :, :GROUP], across,
                preferred_element_type=jnp.float32,
            )
            values = values[: STEP * WINDOW] + values[STEP * WINDOW :] + lax.dot_general(
                top, factor_x[lane, :, GROUP:], across, preferred_element_type=jnp.float32
            )
            for j in range(STEP):
                where = pl.ds(pl.multiple_of((first + j) * rows + start, 8), WINDOW)
                tile[where, :] += values[j * WINDOW : (j + 1) * WINDOW, :]

        return over_windows(bounds, group, visit)

    over_groups(atoms, prepare)


def interpolate_kernel(
    rows, grid, bits, count, bounds, key, charge, fz, fy, fx, tile, force_z, force_y, force_x,
    places, factor_x, table_z, rising_z, total,
):
    force_z[...] = jnp.zeros_like(force_z)
    force_y[...] = jnp.zeros_like(force_y)
    force_x[...] = jnp.zeros_like(force_x)
    fill_places(places)
    atoms = count[0]

    def prepare(group, lane):
        at = pl.ds(pl.multiple_of(group * GROUP, GROUP), GROUP)
        place = group * GROUP + lax.broadcasted_iota(jnp.int32, (1, GROUP), 1)
        value = -jnp.where(place < atoms, charge[0:1, at], 0.0)
        cell_z, cell_y, cell_x = decode(key[0:1, at], *bits)
        weight_z, slope_z = spline_weights(fz[0:1, at])
        weight_y, slope_y = spline_weights(fy[0:1, at])
        weight_x, slope_x = spline_weights(fx[0:1, at])
        for half, values in enumerate((weight_x, slope_x)):
            top, rest = wrapped_stencil(places[...], cell_x, values, grid)
            columns = slice(half * GROUP, (half + 1) * GROUP)
            factor_x[lane, :grid, columns] = top
            factor_x[lane, grid:, columns] = rest
        total[lane] = jnp.zeros(total.shape[1:], jnp.float32)

        def visit(first, start):
            span = table_z.shape[1]
            table_z[lane] = stencil(cell_z - first, weight_z, span)
            rising_z[lane] = stencil(cell_z - first, slope_z, span)
            top, rest = split(
                jnp.concatenate(
                    [
                        tile[pl.ds(pl.multiple_of((first + j) * rows + start, 8), WINDOW), :]
                        for j in range(STEP)
                    ],
                    0,
                )
            )
            along = jnp.dot(
                jnp.concatenate([top, rest], 0), factor_x[lane, :grid, :],
                preferred_element_type=jnp.float32,
            )
            along = along[: STEP * WINDOW] + along[STEP * WINDOW :] + jnp.dot(
                top, factor_x[lane, grid:, :], preferred_element_type=jnp.float32
            )
            table_y = stencil(cell_y - start, weight_y, WINDOW)
            rising_y = stencil(cell_y - start, slope_y, WINDOW)
            zs = [table_z[lane, j : j + 1, :] for j in range(STEP)]
            gs = [rising_z[lane, j : j + 1, :] for j in range(STEP)]
            sums = [0.0, 0.0, 0.0]
            for r in range(0, WINDOW, 8):
                local = slice(r, r + 8)
                w = [along[j * WINDOW + r : j * WINDOW + r + 8, :GROUP] for j in range(STEP)]
                s = [along[j * WINDOW + r : j * WINDOW + r + 8, GROUP:] for j in range(STEP)]
                sums[0] += table_y[local] * sum(gs[j] * w[j] for j in range(STEP))
                sums[1] += rising_y[local] * sum(zs[j] * w[j] for j in range(STEP))
                sums[2] += table_y[local] * sum(zs[j] * s[j] for j in range(STEP))
            for i in range(3):
                total[lane, 8 * i : 8 * i + 8, :] += sums[i]

        rest_of = over_windows(bounds, group, visit)

        def finish():
            rest_of()
            for i, force in enumerate((force_z, force_y, force_x)):
                part = total[lane, 8 * i : 8 * i + 8, :]
                force[0:1, at] = value * jnp.sum(part, 0, keepdims=True)

        return finish

    over_groups(atoms, prepare)


def vmem():
    return pl.BlockSpec(memory_space=pltpu.VMEM)


def smem():
    return pl.BlockSpec(memory_space=pltpu.SMEM)


def spread_atoms(count, bounds, atoms, bits, planes, rows, grid):
    slots = atoms[0].shape[1]
    return pl.pallas_call(
        functools.partial(spread_kernel, rows, grid, bits),
        out_shape=jax.ShapeDtypeStruct((planes * rows, grid), jnp.float32),
        in_specs=[smem()] * 2 + [vmem()] * 5,
        out_specs=vmem(),
        scratch_shapes=[
            pltpu.VMEM((grid, GROUP), jnp.bfloat16),
            pltpu.VMEM((PAIR, 8, GROUP), jnp.float32),
            pltpu.VMEM((PAIR, grid, 2 * GROUP), jnp.bfloat16),
        ],
        cost_estimate=pl.CostEstimate(
            flops=STEP * rows * grid * slots * 6,
            bytes_accessed=planes * rows * grid * 4,
            transcendentals=0,
        ),
        name="spread",
    )(count, bounds, *atoms)


def interpolate_atoms(count, bounds, atoms, tile, bits, planes, rows, grid):
    slots = atoms[0].shape[1]
    return pl.pallas_call(
        functools.partial(interpolate_kernel, rows, grid, bits),
        out_shape=[jax.ShapeDtypeStruct((1, slots), jnp.float32)] * 3,
        in_specs=[smem()] * 2 + [vmem()] * 6,
        out_specs=[vmem()] * 3,
        scratch_shapes=[
            pltpu.VMEM((grid, GROUP), jnp.bfloat16),
            pltpu.VMEM((PAIR, 2 * grid, 2 * GROUP), jnp.bfloat16),
            pltpu.VMEM((PAIR, 8, GROUP), jnp.float32),
            pltpu.VMEM((PAIR, 8, GROUP), jnp.float32),
            pltpu.VMEM((PAIR, 24, GROUP), jnp.float32),
        ],
        cost_estimate=pl.CostEstimate(
            flops=STEP * rows * grid * slots * 12,
            bytes_accessed=planes * rows * grid * 4,
            transcendentals=0,
        ),
        name="interpolate",
    )(count, bounds, *atoms, tile)


def turns(grid, wave, place, quarter):
    whole = np.mod(wave * place + (grid // 4) * quarter, grid)
    return np.cos(2.0 * np.pi * whole / grid).astype(np.float32)


def wave_tables(grid, slabs, columns, waves):
    kx = np.arange(slabs * waves).reshape(slabs, 1, waves)
    part = np.arange(2)
    x = np.arange(grid)
    table_x = turns(grid, kx[None], x[:, None, None, None], part[None, None, :, None])
    kz = np.arange(grid).reshape(columns, 1, grid // columns, 1, 1)
    table_z = turns(
        grid, kz, x[None, None, None, :, None],
        part[None, :, None, None, None] - part[None, None, None, None, :],
    ).reshape(2 * grid, 2 * grid)
    y = np.arange(grid).reshape(columns, 1, grid // columns, 1, 1)
    table_y = turns(
        grid, x[None, None, None, None, :], y,
        part[None, None, None, :, None] - part[None, :, None, None, None],
    )
    return table_x, table_z, table_y


def signed_wave(waves, grid):
    return jnp.where(waves < grid // 2, waves, waves - grid)


def influence(moduli, screening, slab, column, grid, count_kx, count_kz):
    kx = slab * count_kx + lax.iota(jnp.int32, count_kx)
    kz = column * count_kz + lax.iota(jnp.int32, count_kz)
    ky = lax.iota(jnp.int32, grid)
    half = grid // 2
    share = jnp.where((kx == 0) | (kx == half), 1.0, 2.0)
    share = jnp.where(kx <= half, share, 0.0) * (0.5 * coulomb / grid**3)
    nx, nz, ny = (signed_wave(k, grid) for k in (kx, kz, ky))
    radius = (nz * nz)[:, None, None] + (nx * nx)[None, :, None] + (ny * ny)[None, None, :]
    squared = radius.astype(jnp.float32) / float(grid * grid)
    mirrored = jnp.roll(moduli[:, ::-1], 1, 1)
    spare = jnp.zeros((count_kx * lax.axis_size("gz"),), jnp.float32)

    def product(table):
        mx = lax.dynamic_slice_in_dim(
            jnp.concatenate([table[2], spare]), slab * count_kx, count_kx, 0
        )
        mz = lax.dynamic_slice_in_dim(table[0], column * count_kz, count_kz, 0)
        return mz[:, None, None] * (share * mx)[None, :, None] * table[1][None, None, :]

    both = product(moduli) + product(mirrored)
    safe = jnp.where(radius > 0, squared, 1.0)
    return jnp.where(radius > 0, both * jnp.exp(-screening[0] * squared) / safe, 0.0)


def exchange(x, axis):
    return lax.all_to_all(x, axis, split_axis=0, concat_axis=0, tiled=True)


def contract(form, *operands):
    return jnp.einsum(form, *operands, precision=high, preferred_element_type=jnp.float32)


def potential_field(block, kernel, tables, slabs, columns, waves):
    table_x, table_z, table_y = tables
    planes, rows, grid = block.shape
    lanes = waves * rows
    spectrum = contract("zyx,xpck->pzcky", block, table_x)
    spectrum = exchange(spectrum.reshape(slabs * planes * 2, lanes), "gz")
    spectrum = contract("mn,nl->ml", table_z, spectrum)
    spectrum = exchange(spectrum, "gy").reshape(columns, 2, grid // columns, waves, rows)
    spectrum = contract("pczky,pcydw->zkdw", spectrum, table_y)
    spectrum = spectrum * kernel[:, :, None, :]
    spectrum = contract("zkdw,pcydw->pczky", spectrum, table_y)
    spectrum = exchange(spectrum.reshape(2 * grid, lanes), "gy")
    spectrum = contract("mn,ml->nl", table_z, spectrum)
    spectrum = exchange(spectrum, "gz").reshape(slabs, planes, 2, waves, rows)
    return contract("pzcky,xpck->zyx", spectrum, table_x)


LANES = 128
MESH = pl.DeviceIdType.MESH


def fast_sizes(slabs, columns, planes, rows, grid):
    return (
        2 * rows == LANES
        and grid == 2 * LANES
        and columns * rows == grid
        and slabs * planes == grid
        and planes % 4 == 0
        and slabs >= 3
        and columns >= 3
    )


def green_rows(moduli, screening, slab, column, grid, count_kx, columns):
    half = grid // 2
    share_kz = half // columns
    kx = slab * count_kx + lax.iota(jnp.int32, count_kx)
    part = lax.broadcasted_iota(jnp.int32, (2, share_kz), 0)
    kz = part * half + column * share_kz + lax.broadcasted_iota(jnp.int32, (2, share_kz), 1)
    ky = lax.iota(jnp.int32, grid)
    share = jnp.where((kx == 0) | (kx == half), 1.0, 2.0)
    share = jnp.where(kx <= half, share, 0.0) * (0.5 * coulomb / grid**3)
    nx, nz, ny = (signed_wave(k, grid) for k in (kx, kz, ky))
    radius = (nx * nx)[:, None, None, None] + (nz * nz)[None, :, :, None] + (ny * ny)
    squared = radius.astype(jnp.float32) / float(grid * grid)
    mirrored = jnp.roll(moduli[:, ::-1], 1, 1)
    spare = jnp.zeros((count_kx * lax.axis_size("gz"),), jnp.float32)

    def product(table):
        mx = lax.dynamic_slice_in_dim(
            jnp.concatenate([table[2], spare]), slab * count_kx, count_kx, 0
        )
        mz = lax.dynamic_slice_in_dim(table[0].reshape(2, half), column * share_kz, share_kz, 1)
        return (share * mx)[:, None, None, None] * mz[None, :, :, None] * table[1]

    both = product(moduli) + product(mirrored)
    safe = jnp.where(radius > 0, squared, 1.0)
    green = jnp.where(radius > 0, both * jnp.exp(-screening[0] * squared) / safe, 0.0)
    return green.reshape(count_kx * grid // columns, grid)


def halves(table):
    table = np.ascontiguousarray(table, dtype=np.float32)
    top = table.astype(jnp.bfloat16)
    rest = (table - top.astype(np.float32)).astype(jnp.bfloat16)
    return top, rest


def solve_tables(grid, slabs, columns, waves, planes):
    half = grid // 2
    pairs = planes // 2
    share = half // columns
    x = np.arange(grid)
    part = np.arange(2)
    kx = np.repeat(np.arange(slabs * waves), 2)
    px = np.tile(part, slabs * waves)
    table_x = turns(grid, kx[:, None], x[None, :], px[:, None])
    top, rest = halves(table_x)
    forward_x = np.stack([top, rest])
    top, rest = halves(table_x.T)
    pad = round_up(3 * top.shape[1], LANES) - 3 * top.shape[1]
    inverse_x = np.concatenate([top, rest, top, np.zeros((grid, pad), top.dtype)], 1)
    kz = np.broadcast_to(np.arange(half).reshape(columns, 1, share), (columns, 2, share)).reshape(-1)
    pk = np.broadcast_to(part.reshape(1, 2, 1), (columns, 2, share)).reshape(-1)
    zh = np.broadcast_to(np.arange(half).reshape(slabs, 1, pairs), (slabs, 2, pairs)).reshape(-1)
    pz = np.broadcast_to(part.reshape(1, 2, 1), (slabs, 2, pairs)).reshape(-1)
    table_z = turns(half, kz[:, None], zh[None, :], pk[:, None] - pz[None, :])
    forward_z = np.stack(halves(table_z))
    inverse_z = np.stack(halves(table_z.T))
    ky = np.tile(np.arange(grid), 2)
    pf = np.repeat(part, grid)
    table_y = turns(grid, ky[:, None], ky[None, :], pf[None, :] - pf[:, None])
    forward_y = np.stack(halves(table_y))
    angle = 2.0 * np.pi * np.arange(half)[:, None] / grid
    upper = np.arange(LANES)[None, :] >= LANES // 2
    twist = np.stack(
        [np.where(upper, np.cos(angle), 1.0), np.where(upper, np.sin(angle), 0.0)]
    ).astype(np.float32)
    return forward_x, inverse_x, forward_z, inverse_z, forward_y, twist


def chunks_of(waves, count):
    edges = [waves * i // count for i in range(count + 1)]
    return [(a, b - a) for a, b in zip(edges, edges[1:]) if b > a]


def solve_kernel(
    slabs, columns, waves, planes, rows, grid, chunks,
    tile, green, table_fx, table_ix, table_fz, table_iz, table_y, twist, out,
    rim_z, rim_y, rim_c, block, fx, fz, iz, fy, iy,
    x_out, z_in, z_out, y_in, y_out, z_back, z_send, x_in, potential, y_left, y_right,
    rim_send, rim_recv, gz_send, gz_recv, gy_send, gy_recv, by_send, by_recv, bz_send, bz_recv,
):
    half = grid // 2
    pairs = planes // 2
    wide = 2 * pairs
    share = half // columns
    tall = 2 * share
    bins = 2 * slabs * waves
    slab = lax.axis_index("gz")
    column = lax.axis_index("gy")

    def around(step):
        return lax.rem(slab + step + slabs, slabs)

    def beside(step):
        return lax.rem(column + step + columns, columns)

    barrier = pltpu.get_barrier_semaphore()
    for step in range(1, slabs):
        pl.semaphore_signal(barrier, inc=1, device_id=(around(step), column), device_id_type=MESH)
    for step in range(1, columns):
        pl.semaphore_signal(barrier, inc=1, device_id=(slab, beside(step)), device_id_type=MESH)
    for step in (1, -1):
        pl.semaphore_signal(
            barrier, inc=1, device_id=(around(step), beside(step)), device_id_type=MESH
        )
    pl.semaphore_wait(barrier, slabs + columns)

    def remote(source, target, sends, recvs, at, to):
        return pltpu.make_async_remote_copy(
            src_ref=source, dst_ref=target, send_sem=sends.at[at], recv_sem=recvs.at[at],
            device_id=to, device_id_type=MESH,
        )

    main, edge = pl.ds(0, rows), pl.ds(rows, 8)
    body_z, over_z = pl.ds(0, planes), pl.ds(planes, 3)
    rims = [
        remote(tile.at[over_z, main], rim_z, rim_send, rim_recv, 0, (around(1), column)),
        remote(tile.at[body_z, edge], rim_y, rim_send, rim_recv, 1, (slab, beside(1))),
        remote(tile.at[over_z, edge], rim_c, rim_send, rim_recv, 2, (around(1), beside(1))),
    ]
    for copy in rims:
        copy.start()

    for source, target in ((table_fx, fx), (table_fz, fz), (table_iz, iz)):
        size = source.shape[2]
        target[:, :size] = source[0]
        target[:, size : 2 * size] = source[1]
        target[:, 2 * size :] = source[0]
    size = 2 * grid
    fy[:size, :] = table_y[0]
    fy[size : 2 * size, :] = table_y[0]
    fy[2 * size :, :] = table_y[1]
    iy[:, :size] = table_y[0]
    iy[:, size : 2 * size] = table_y[0]
    iy[:, 2 * size :] = table_y[1]
    potential[planes + 3 :] = jnp.zeros_like(potential[planes + 3 :])

    for copy in rims:
        copy.wait()

    def add_rims(at):
        block[pl.ds(at * 4, 4)] = tile[pl.ds(at * 4, 4), :rows, :]
        block[pl.ds(at * 4, 4), :8, :] += rim_y[pl.ds(at * 4, 4)]

    pl.loop(0, planes // 4)(add_rims)
    rim_z[:, :8, :] += rim_c[...]
    block[:3] += rim_z[...]

    def along_x(at):
        top, rest = split(block[pl.ds(at * 4, 4)].reshape(4 * rows, grid))
        values = lax.dot_general(
            fx[...], jnp.concatenate([top, top, rest], 1), (((1,), (1,)), ((), ())),
            preferred_element_type=jnp.float32,
        )
        for side in range(2):
            where = pl.ds(2 * at + side, bins, stride=pairs)
            x_out[where, :] = values[:, side * LANES : (side + 1) * LANES]

    pl.loop(0, planes // 4)(along_x)

    def gz_copy(q, step):
        w, n = chunks[q]
        source = x_out.at[pl.ds((around(step) * waves + w) * wide, n * wide)]
        target = z_in.at[slab, pl.ds(w * wide, n * wide)]
        return remote(source, target, gz_send, gz_recv, (q, step), (around(step), column))

    def gy_copy(q, step):
        w, n = chunks[q]
        where = pl.ds(w * tall, n * tall)
        source, target = z_out.at[beside(step), where], y_in.at[column, where]
        return remote(source, target, gy_send, gy_recv, (q, step), (slab, beside(step)))

    def by_copy(q, step):
        w, n = chunks[q]
        where = pl.ds(w * tall, n * tall)
        source, target = y_out.at[beside(step), where], z_back.at[column, where]
        return remote(source, target, by_send, by_recv, (q, step), (slab, beside(step)))

    def bz_copy(q, step):
        w, n = chunks[q]
        source = z_send.at[around(step), pl.ds(w * wide, n * wide)]
        target = x_in.at[pl.ds((slab * waves + w) * wide, n * wide)]
        return remote(source, target, bz_send, bz_recv, (q, step), (around(step), column))

    for q in range(len(chunks)):
        for step in range(1, slabs):
            gz_copy(q, step).start()
    z_in[slab] = x_out[pl.ds(pl.multiple_of(slab * waves * wide, wide), waves * wide), :]

    left = lax.broadcasted_iota(jnp.int32, (half, LANES), 1) < LANES // 2
    side = left[:share]

    def turn(value):
        return pltpu.roll(value, LANES // 2, 1)

    def three(value):
        top, rest = split(value)
        return jnp.concatenate([top, top, rest], 0)

    def to_z(q):
        for step in range(1, slabs):
            gz_copy(q, step).wait_recv()
        first, count = chunks[q]

        @pl.loop(first, first + count)
        def _(w):
            value = z_in[:, pl.ds(pl.multiple_of(w * wide, wide), wide), :].reshape(grid, LANES)
            value = jnp.dot(fz[...], three(value), preferred_element_type=jnp.float32)
            value = value.reshape(columns, 2, share, LANES)
            re = value[:, 0].reshape(half, LANES)
            im = value[:, 1].reshape(half, LANES)
            re, im = re * twist[0] + im * twist[1], im * twist[0] - re * twist[1]
            for p, v in enumerate((re, im)):
                v = jnp.where(left, v + turn(v), turn(v) - v)
                where = pl.ds(pl.multiple_of(w * tall + p * share, share), share)
                z_out[:, where, :] = v.reshape(columns, share, LANES)

        for step in range(1, columns):
            gy_copy(q, step).start()
        where = pl.ds(first * tall, count * tall)
        y_in[column, where, :] = z_out[column, where, :]

    def to_y(q):
        for step in range(1, columns):
            gy_copy(q, step).wait_recv()
        first, count = chunks[q]
        size = 2 * grid

        @pl.loop(0, count)
        def _(w):
            for p in range(2):
                where = pl.ds(pl.multiple_of((first + w) * tall + p * share, share), share)
                for c in range(0, columns, 2):
                    a, b = y_in[c, where, :], y_in[c + 1, where, :]
                    pair = (jnp.where(side, a, turn(b)), jnp.where(side, turn(a), b))
                    for h in range(2):
                        to = pl.ds(pl.multiple_of(w * tall + h * share, share), share)
                        at = (p * columns + c) * rows
                        top, rest = split(pair[h])
                        y_left[to, at : at + LANES] = top
                        y_left[to, size + at : size + at + LANES] = rest
                        y_left[to, 2 * size + at : 2 * size + at + LANES] = top

        value = jnp.dot(y_left[: count * tall, :], fy[...], preferred_element_type=jnp.float32)
        factor = green[first * tall : (first + count) * tall, :]
        value = jnp.concatenate([value[:, :grid] * factor, value[:, grid:] * factor], 1)
        top, rest = split(value)
        y_right[: count * tall, :] = lax.dot_general(
            jnp.concatenate([top, rest, top], 1), iy[...], (((1,), (1,)), ((), ())),
            preferred_element_type=jnp.float32,
        )

        @pl.loop(0, count)
        def _(w):
            for p in range(2):
                where = pl.ds(pl.multiple_of((first + w) * tall + p * share, share), share)
                for c in range(0, columns, 2):
                    at = (p * columns + c) * rows
                    a, b = (
                        y_right[
                            pl.ds(pl.multiple_of(w * tall + h * share, share), share),
                            at : at + LANES,
                        ]
                        for h in range(2)
                    )
                    y_out[c, where, :] = jnp.where(side, a, turn(b))
                    y_out[c + 1, where, :] = jnp.where(side, turn(a), b)

        for step in range(1, columns):
            by_copy(q, step).start()
        where = pl.ds(first * tall, count * tall)
        z_back[column, where, :] = y_out[column, where, :]

    def from_z(q):
        for step in range(1, columns):
            by_copy(q, step).wait_recv()
        first, count = chunks[q]

        @pl.loop(first, first + count)
        def _(w):
            value = z_back[:, pl.ds(pl.multiple_of(w * tall, tall), tall), :]
            re = value[:, :share].reshape(half, LANES)
            im = value[:, share:].reshape(half, LANES)
            re, im = (jnp.where(left, v + turn(v), turn(v) - v) for v in (re, im))
            re, im = re * twist[0] - im * twist[1], im * twist[0] + re * twist[1]
            re, im = (v.reshape(columns, share, LANES) for v in (re, im))
            value = jnp.concatenate(
                [v[c] for c in range(columns) for v in (re, im)], 0
            )
            value = jnp.dot(iz[...], three(value), preferred_element_type=jnp.float32)
            where = pl.ds(pl.multiple_of(w * wide, wide), wide)
            z_send[:, where, :] = value.reshape(slabs, wide, LANES)

        for step in range(1, slabs):
            bz_copy(q, step).start()
        where = pl.ds(pl.multiple_of((slab * waves + first) * wide, wide), count * wide)
        x_in[where, :] = z_send[slab, pl.ds(first * wide, count * wide), :]

    stages = (to_z, to_y, from_z)
    for turn_at in range(len(chunks) + len(stages) - 1):
        for at, stage in enumerate(stages):
            if 0 <= turn_at - at < len(chunks):
                stage(turn_at - at)
    for q in range(len(chunks)):
        for step in range(1, slabs):
            bz_copy(q, step).wait_recv()

    spare = table_ix.shape[1] - 3 * bins

    def back_x(at):
        value = jnp.concatenate(
            [x_in[pl.ds(2 * at + s, bins, stride=pairs), :] for s in range(2)], 1
        )
        top, rest = split(value)
        stack = [top, top, rest]
        if spare:
            stack.append(jnp.zeros((spare, 2 * LANES), jnp.bfloat16))
        value = jnp.dot(
            table_ix[...], jnp.concatenate(stack, 0), preferred_element_type=jnp.float32
        )
        potential[pl.ds(at * 4, 4), :rows, :] = value.T.reshape(4, rows, grid)

    pl.loop(0, planes // 4)(back_x)
    rims_back = [
        remote(
            potential.at[pl.ds(0, 3), main], potential.at[over_z, main],
            rim_send, rim_recv, 3, (around(-1), column),
        ),
        remote(
            potential.at[body_z, pl.ds(0, 8)], potential.at[body_z, edge],
            rim_send, rim_recv, 4, (slab, beside(-1)),
        ),
        remote(
            potential.at[pl.ds(0, 3), pl.ds(0, 8)], potential.at[over_z, edge],
            rim_send, rim_recv, 5, (around(-1), beside(-1)),
        ),
    ]
    for copy in rims_back:
        copy.start()
    for q in range(len(chunks)):
        for copy, steps in (
            (gz_copy, slabs), (gy_copy, columns), (by_copy, columns), (bz_copy, slabs)
        ):
            for step in range(1, steps):
                copy(q, step).wait_send()
    for copy in rims_back:
        copy.wait()

    def give(at):
        out[pl.ds(at * 4, 4)] = potential[pl.ds(at * 4, 4)]

    pl.loop(0, out.shape[0] // 4)(give)


def solve_fused(tile, green, slabs, columns, planes, rows, waves):
    span_planes, span_rows, grid = tile.shape
    tables = solve_tables(grid, slabs, columns, waves, planes)
    chunks = chunks_of(waves, CHUNKS)
    most = max(n for _, n in chunks)
    wide, tall = planes, 2 * (grid // 2 // columns)
    bins = 2 * slabs * waves

    def scratch(*shape):
        return pltpu.VMEM(shape, jnp.float32)

    def narrow(*shape):
        return pltpu.VMEM(shape, jnp.bfloat16)

    def flags(count):
        return [pltpu.SemaphoreType.DMA((len(chunks), count))] * 2

    return pl.pallas_call(
        functools.partial(
            solve_kernel, slabs, columns, waves, planes, rows, grid, chunks
        ),
        out_shape=jax.ShapeDtypeStruct(tile.shape, jnp.float32),
        in_specs=[vmem()] * 8,
        out_specs=vmem(),
        scratch_shapes=[
            scratch(3, rows, grid), scratch(planes, 8, grid), scratch(3, 8, grid),
            scratch(planes, rows, grid),
            narrow(bins, 3 * grid), narrow(grid, 3 * grid), narrow(grid, 3 * grid),
            narrow(6 * grid, 2 * grid), narrow(2 * grid, 6 * grid),
            scratch(slabs * waves * wide, LANES), scratch(slabs, waves * wide, LANES),
            scratch(columns, waves * tall, LANES), scratch(columns, waves * tall, LANES),
            scratch(columns, waves * tall, LANES), scratch(columns, waves * tall, LANES),
            scratch(slabs, waves * wide, LANES), scratch(slabs * waves * wide, LANES),
            scratch(*tile.shape),
            narrow(most * tall, 6 * grid), scratch(most * tall, 2 * grid),
            pltpu.SemaphoreType.DMA((6,)), pltpu.SemaphoreType.DMA((6,)),
            *flags(slabs), *flags(columns), *flags(columns), *flags(slabs),
        ],
        compiler_params=pltpu.CompilerParams(
            collective_id=0, has_side_effects=True, vmem_limit_bytes=60 * 1024 * 1024
        ),
        cost_estimate=pl.CostEstimate(
            flops=10**10, bytes_accessed=span_planes * span_rows * grid * 8, transcendentals=0
        ),
        name="solve",
    )(tile, green, *(jnp.asarray(t) for t in tables))


def solve_tile(volume, kernel, tables, planes, rows, waves, slabs, columns):
    span_planes, span_rows, grid = volume.shape
    rim_planes = shifted(volume[planes : planes + 3], "gz", 1)
    volume = jnp.concatenate([volume[:3] + rim_planes, volume[3:planes]], 0)
    rim_rows = shifted(volume[:, rows : rows + 3], "gy", 1)
    block = jnp.concatenate([volume[:, :3] + rim_rows, volume[:, 3:rows]], 1)
    potential = potential_field(block, kernel, tables, slabs, columns, waves)
    upper_rows = shifted(potential[:, :3], "gy", -1)
    spare_rows = jnp.zeros((planes, span_rows - rows - 3, grid), jnp.float32)
    widened = jnp.concatenate([potential, upper_rows, spare_rows], 1)
    upper_planes = shifted(widened[:3], "gz", -1)
    spare_planes = jnp.zeros((span_planes - planes - 3, span_rows, grid), jnp.float32)
    return jnp.concatenate([widened, upper_planes, spare_planes], 0)


def body(charge, fractions, cell_base, live_blocks, send_blocks, moduli, screening):
    slabs = lax.axis_size("gz")
    columns = lax.axis_size("gy")
    grid = moduli.shape[1]
    planes = grid // slabs
    rows = grid // columns
    span_planes = round_up(planes + 3 + STEP, 2)
    span_rows = round_up(rows + 3, 8)
    waves = -(-(grid // 2 + 1) // slabs)
    slab = lax.axis_index("gz")
    column = lax.axis_index("gy")
    lane_ids = lax.iota(jnp.int32, columns)
    live = jnp.sum(jnp.where(lane_ids == column, live_blocks[0], 0))
    send = jnp.sum(jnp.where(lane_ids == column, send_blocks[0], 0))
    kept_atoms = (live - send) * BLOCK
    live_atoms = live * BLOCK
    slots = charge.shape[0]
    bits = ((rows - 1).bit_length(), (grid - 1).bit_length())
    slot = lax.iota(jnp.int32, slots)
    key = jnp.where(slot < live_atoms, encode(cell_base, *bits), DEAD)
    key, slot, *values = lax.sort(
        (key, slot, charge, fractions[0], fractions[1], fractions[2]),
        num_keys=1, is_stable=False,
    )
    by_group = key.reshape(slots // GROUP, GROUP)
    alive = by_group < DEAD
    cell_z, cell_y, _ = decode(by_group, *bits)
    bounds = []
    for cell in (cell_z, cell_y):
        high = jnp.max(jnp.where(alive, cell, 0), 1)
        bounds += [jnp.min(jnp.where(alive, cell, high[:, None]), 1), high]
    bounds = jnp.stack(bounds)
    atoms = [v[None, :] for v in (key, *values)]
    sizes = (span_planes, span_rows, grid)
    count = live_atoms[None]
    tile = spread_atoms(count, bounds, atoms, bits, *sizes).reshape(sizes)
    if fast_sizes(slabs, columns, planes, rows, grid):
        green = green_rows(moduli, screening, slab, column, grid, waves, columns)
        padded = solve_fused(tile, green, slabs, columns, planes, rows, waves)
    else:
        tables = wave_tables(grid, slabs, columns, waves)
        kernel = influence(moduli, screening, slab, column, grid, waves, grid // columns)
        padded = solve_tile(tile, kernel, tables, planes, rows, waves, slabs, columns)
    padded = padded.reshape(span_planes * span_rows, grid)
    forces = interpolate_atoms(count, bounds, atoms, padded, bits, *sizes)
    _, *home = lax.sort((slot, *(f[0] for f in forces)), num_keys=1, is_stable=False)
    home = jnp.stack(home)
    margin = SEND_MAX * BLOCK
    room = jnp.concatenate([home, jnp.zeros((3, margin), jnp.float32)], 1)
    lent = lax.dynamic_slice_in_dim(room, kept_atoms, margin, 1)
    moved = shifted(lent, "gy", 1)
    kept = jnp.where(lax.iota(jnp.int32, slots) < kept_atoms, home, 0.0)
    holder = jnp.zeros((3, slots + margin), jnp.float32)
    holder = lax.dynamic_update_slice(holder, moved, (jnp.zeros((), jnp.int32), kept_atoms))
    return kept + holder[:, :slots]


def solution(mesh):
    return jax.shard_map(
        body,
        mesh=mesh,
        in_specs=(
            P(("gz", "gy")),
            P(None, ("gz", "gy")),
            P(None, ("gz", "gy")),
            P("gz", None),
            P("gz", None),
            P(),
            P(),
        ),
        out_specs=P(None, ("gz", "gy")),
        check_vma=False,
    )
```

profile of v0, /device:TPU:26, one launch (start us, length us, event | category | flops | bytes accessed | tf_op | source)
XLA Modules:
  0.0 201.5 jit_solution(13086097454584707679)
XLA Ops:
  0.0 0.0 copy-start.1
  0.0 0.0 slice-start
  0.0 1.3 shift-left_or_fusion
  1.3 1.3 fusion.16
  2.6 1.3 fusion.11
  4.6 13.0 %sort.66 = (s32[12288]{0:T(1024)S(1)}, s32[12288]{0:T(1024)S(1)}, f32[12288]{0:T(1024)}, f32[12288]{0:T(1024)}, f32[12288]{0:T(1024)}, /*index=5*/f32[12288]{0:T(1024)}) sort(s32[12288]{0:T(1024)S(1)} %fusion.7, s32[12288]{0:T(1024)S(1)} %iota.37, f32[12288]{0:T(1024)} %param.13, f32[12288]{0:T(1024)S(1)} %bitcast.35, f32[12288]{0:T(1024)S(1)} %bitcast.36, ...), dimensions={0}, to_apply=%region_2.3 | sort | flops 172032 | bytes 589824 | tf_op jit(solution)/shard_map/sort | solution.py:820
  17.6 0.0 copy-start
  17.6 0.0 copy-done.1
  17.6 0.1 slice.62
  17.8 0.2 reverse.2
  18.0 0.1 slice.73
  18.1 0.0 slice-done
  18.1 0.1 pad_maximum_fusion.3
  18.2 0.1 fusion.14
  18.3 0.1 constant_dynamic-slice_fusion
  18.3 0.1 broadcast_multiply_fusion.1
  18.4 0.1 mul.166
  18.5 0.1 broadcast_multiply_fusion
  18.6 0.1 mul.175
  18.7 0.1 fusion.8
  18.8 0.1 broadcast_add_fusion
  18.8 0.1 add.108
  19.6 0.1 select_reduce_fusion.3
  19.7 0.2 select_reduce_fusion.2
  19.9 0.6 pad_add_fusion.bounds
  20.5 0.0 copy-done
  20.5 16.6 %spread.1 = f32[3024,256]{1,0:T(8,128)} custom-call(s32[1]{0:T(128)} %bitcast.6.count, s32[4,48]{1,0:T(4,128)} %pad_add_fusion.bounds, s32[1,12288]{1,0:T(1,128)} %bitcast.38, f32[1,12288]{1,0:T(1,128)} %bitcast.60, f32[1,12288]{1,0:T(1,128)} %bitcast.62, f32[1,12288]{1,0:T(1,128)} %bitcast.64, f32[1,12288]{1,0:T(1,128)} %bitcast.66), custom_call_target="tpu_custom_call" | custom-call | flops 9512681472 | bytes 3096576 | tf_op jit(solution)/shard_map/spread/pallas_call | solution.py:249
  37.1 1.7 fusion.2.green
  38.8 126.9 %solve.1 = f32[42,72,256]{2,1,0:T(8,128)} custom-call(f32[42,72,256]{2,1,0:T(8,128)} %bitcast.69, f32[1088,256]{1,0:T(8,128)} %fusion.2.green, bf16[2,272,256]{2,1,0:T(8,128)(2,1)} %constant.26.clone.table_fx, bf16[256,896]{1,0:T(8,128)(2,1)} %constant.27.clone.table_ix, bf16[2,256,256]{2,1,0:T(8,128)(2,1)} %constant.28.clone.table_fz, ...), custom_call_target="tpu_custom_call" | custom-call | flops 10000000000 | bytes 6193152 | tf_op jit(solution)/shard_map/solve/pallas_call | solution.py:754
  165.7 21.2 %interpolate.1 = (f32[1,12288]{1,0:T(1,128)}, f32[1,12288]{1,0:T(1,128)}, f32[1,12288]{1,0:T(1,128)}) custom-call(s32[1]{0:T(128)} %bitcast.6.count, s32[4,48]{1,0:T(4,128)} %pad_add_fusion.bounds, s32[1,12288]{1,0:T(1,128)} %bitcast.39, f32[1,12288]{1,0:T(1,128)} %bitcast.61, f32[1,12288]{1,0:T(1,128)} %bitcast.63, f32[1,12288]{1,0:T(1,128)} %bitcast.65, ...), custom_call_target="tpu_custom_call" | custom-call | flops 19025362944 | bytes 3096576 | tf_op jit(solution)/shard_map/interpolate/pallas_call | solution.py:270
  188.0 8.5 %sort.67 = (s32[12288]{0:T(1024)}, f32[12288]{0:T(1024)S(1)}, f32[12288]{0:T(1024)S(1)}, f32[12288]{0:T(1024)S(1)}) sort(s32[12288]{0:T(1024)S(1)} %get-tuple-element.17, f32[12288]{0:T(1024)} %bitcast.46, f32[12288]{0:T(1024)} %bitcast.47, f32[12288]{0:T(1024)} %bitcast.48), dimensions={0}, to_apply=%region_7.8 | sort | flops 172032 | bytes 393216 | tf_op jit(solution)/shard_map/sort | solution.py:845
  196.5 0.1 pad_maximum_fusion
  196.6 0.1 pad_dynamic-slice_fusion
  196.7 0.1 collective-permute-start
  196.8 3.7 %collective-permute-done = f32[3,4608]{1,0:T(4,128)S(1)} collective-permute-done((f32[3,4608]{1,0:T(4,128)S(1)}, f32[3,4608]{1,0:T(4,128)S(1)}, u32[]{:S(2)}, u32[]{:S(2)}) %collective-permute-start) | collective-permute-done | bytes 55328 | tf_op jit(solution)/shard_map/ppermute | solution.py:27
  200.6 0.9 slice_add_fusion
  (14 shorter events, 0.2 us)
Async XLA Ops:
  0.0 17.6 %copy-start.1 = (f32[3,256]{1,0:T(4,128)S(1)}, f32[3,256]{1,0:T(4,128)}, u32[]{:S(2)}) copy-start(f32[3,256]{1,0:T(4,128)} %param.18) | copy-start | bytes 9220
  0.0 18.1 %slice-start = ((f32[3,256]{1,0:T(4,128)}), f32[3,1]{1,0:T(4,128)S(1)}, s32[]{:S(2)}) async-start(f32[3,256]{1,0:T(4,128)} %param.18), calls=%async_computation | async-start | bytes 4096 | tf_op jit(solution)/shard_map/jit(_roll_static)/slice | solution.py:396
  17.6 2.9 %copy-start = (s32[12288]{0:T(1024)}, s32[12288]{0:T(1024)S(1)}, u32[]{:S(2)}) copy-start(s32[12288]{0:T(1024)S(1)} %get-tuple-element.18) | copy-start | bytes 147460
  196.7 3.8 %collective-permute-start = (f32[3,4608]{1,0:T(4,128)S(1)}, f32[3,4608]{1,0:T(4,128)S(1)}, u32[]{:S(2)}, u32[]{:S(2)}) collective-permute-start(f32[3,4608]{1,0:T(4,128)S(1)} %pad_dynamic-slice_fusion), channel_id=1, source_target_pairs={{0,1},{1,2},{2,3},{3,0},{4,5},{5,6},{6,7},{7,4},{8,9},{9,10},{10,1... | collective-permute-start | bytes 165896 | tf_op jit(solution)/shard_map/ppermute | solution.py:27
where the time goes:
time: 205 us; the launch traced here: 202 us
  Pallas kernels  165 us (80%)
  other arithmetic  28.3 us (14%)
  waiting for transfers between devices  3.74 us (2%)
  between operations  2.61 us (1%)
  local copies, waits for them, and re-layouts  2.15 us (1%)
    pallas_call x1, Pallas kernels, solve_fused(): pl.pallas_call(functools.partial(solve_kernel, slabs, columns, waves, pla...  127 us
    pallas_call x1, Pallas kernels, interpolate_atoms(): pl.pallas_call(functools.partial(interpolate_kernel, rows, grid, bits), o...  21.2 us
    pallas_call x1, Pallas kernels, spread_atoms(): pl.pallas_call(functools.partial(spread_kernel, rows, grid, bits), out_sh...  16.6 us
    sort x1, other arithmetic, body(): lax.sort((key, slot, charge, fractions[0], fractions[1], fractions[2]), n...  13 us
    sort x1, other arithmetic, body(): lax.sort((slot, *(f[0] for f in forces)), num_keys=1, is_stable=False)  8.48 us
  transfers between devices with their start and end apart: 1, of which 1 were waited for; matrix products, arithmetic and copies ran while one was open for 0% of the time, Pallas kernels for 0%

commit v1 on v0

--- a/solution.py
+++ b/solution.py
@@ -99,7 +99,7 @@
 
 
 def over_windows(bounds, group, visit):
-    low_z, high_z, low_y, high_y = (bounds[i, group] for i in range(4))
+    low_z, high_z, low_y, high_y = (bound[group] for bound in bounds)
     start = (low_y // 8) * 8
     steps = (high_z + 3 - low_z) // STEP + 1
     strips = (high_y + 3 - start) // WINDOW + 1
@@ -122,7 +122,7 @@
 
 
 def spread_kernel(
-    rows, grid, bits, count, bounds, key, charge, fz, fy, fx, tile, places, table_z, factor_x,
+    rows, grid, bits, count, low_z, high_z, low_y, high_y, key, charge, fz, fy, fx, tile, places, table_z, factor_x,
 ):
     tile[...] = jnp.zeros_like(tile)
     fill_places(places)
@@ -158,13 +158,13 @@
                 where = pl.ds(pl.multiple_of((first + j) * rows + start, 8), WINDOW)
                 tile[where, :] += values[j * WINDOW : (j + 1) * WINDOW, :]
 
-        return over_windows(bounds, group, visit)
+        return over_windows((low_z, high_z, low_y, high_y), group, visit)
 
     over_groups(atoms, prepare)
 
 
 def interpolate_kernel(
-    rows, grid, bits, count, bounds, key, charge, fz, fy, fx, tile, force_z, force_y, force_x,
+    rows, grid, bits, count, low_z, high_z, low_y, high_y, key, charge, fz, fy, fx, tile, force_z, force_y, force_x,
     places, factor_x, table_z, rising_z, total,
 ):
     force_z[...] = jnp.zeros_like(force_z)
@@ -223,7 +223,7 @@
             for i in range(3):
                 total[lane, 8 * i : 8 * i + 8, :] += sums[i]
 
-        rest_of = over_windows(bounds, group, visit)
+        rest_of = over_windows((low_z, high_z, low_y, high_y), group, visit)
 
         def finish():
             rest_of()
@@ -249,7 +249,7 @@
     return pl.pallas_call(
         functools.partial(spread_kernel, rows, grid, bits),
         out_shape=jax.ShapeDtypeStruct((planes * rows, grid), jnp.float32),
-        in_specs=[smem()] * 2 + [vmem()] * 5,
+        in_specs=[smem()] * 5 + [vmem()] * 5,
         out_specs=vmem(),
         scratch_shapes=[
             pltpu.VMEM((grid, GROUP), jnp.bfloat16),
@@ -262,7 +262,7 @@
             transcendentals=0,
         ),
         name="spread",
-    )(count, bounds, *atoms)
+    )(count, *bounds, *atoms)
 
 
 def interpolate_atoms(count, bounds, atoms, tile, bits, planes, rows, grid):
@@ -270,7 +270,7 @@
     return pl.pallas_call(
         functools.partial(interpolate_kernel, rows, grid, bits),
         out_shape=[jax.ShapeDtypeStruct((1, slots), jnp.float32)] * 3,
-        in_specs=[smem()] * 2 + [vmem()] * 6,
+        in_specs=[smem()] * 5 + [vmem()] * 6,
         out_specs=[vmem()] * 3,
         scratch_shapes=[
             pltpu.VMEM((grid, GROUP), jnp.bfloat16),
@@ -285,7 +285,7 @@
             transcendentals=0,
         ),
         name="interpolate",
-    )(count, bounds, *atoms, tile)
+    )(count, *bounds, *atoms, tile)
 
 
 def turns(grid, wave, place, quarter):
@@ -375,38 +375,79 @@
         and grid == 2 * LANES
         and columns * rows == grid
         and slabs * planes == grid
-        and planes % 4 == 0
+        and planes % 8 == 0
+        and LANES % (2 * columns) == 0
+        and LANES % slabs == 0
         and slabs >= 3
         and columns >= 3
     )
 
 
-def green_rows(moduli, screening, slab, column, grid, count_kx, columns):
+def kept_waves(half, columns):
+    pairs = [k for n in range(1, half // 2) for k in (n, half - n)]
+    return np.array([0, half // 2] + pairs).reshape(columns, half // columns)
+
+
+def partners(half, columns):
+    share = half // columns
+    moves = np.zeros((columns, 2 * share, 2 * share), np.float32)
+    for c, waves in enumerate(kept_waves(half, columns)):
+        place = {int(k): j for j, k in enumerate(waves)}
+        for h in range(2):
+            for k, j in place.items():
+                other = (2 * half - h * half - k) % (2 * half)
+                moves[c, h * share + j, other // half * share + place[other % half]] = 1.0
+    return moves.astype(jnp.bfloat16)
+
+
+def fill_green(green, moduli, screening, slab, column, waves, columns):
+    grid = moduli.shape[1]
     half = grid // 2
-    share_kz = half // columns
-    kx = slab * count_kx + lax.iota(jnp.int32, count_kx)
-    part = lax.broadcasted_iota(jnp.int32, (2, share_kz), 0)
-    kz = part * half + column * share_kz + lax.broadcasted_iota(jnp.int32, (2, share_kz), 1)
-    ky = lax.iota(jnp.int32, grid)
-    share = jnp.where((kx == 0) | (kx == half), 1.0, 2.0)
-    share = jnp.where(kx <= half, share, 0.0) * (0.5 * coulomb / grid**3)
-    nx, nz, ny = (signed_wave(k, grid) for k in (kx, kz, ky))
-    radius = (nx * nx)[:, None, None, None] + (nz * nz)[None, :, :, None] + (ny * ny)
-    squared = radius.astype(jnp.float32) / float(grid * grid)
-    mirrored = jnp.roll(moduli[:, ::-1], 1, 1)
-    spare = jnp.zeros((count_kx * lax.axis_size("gz"),), jnp.float32)
-
-    def product(table):
-        mx = lax.dynamic_slice_in_dim(
-            jnp.concatenate([table[2], spare]), slab * count_kx, count_kx, 0
-        )
-        mz = lax.dynamic_slice_in_dim(table[0].reshape(2, half), column * share_kz, share_kz, 1)
-        return (share * mx)[:, None, None, None] * mz[None, :, :, None] * table[1]
-
-    both = product(moduli) + product(mirrored)
-    safe = jnp.where(radius > 0, squared, 1.0)
-    green = jnp.where(radius > 0, both * jnp.exp(-screening[0] * squared) / safe, 0.0)
-    return green.reshape(count_kx * grid // columns, grid)
+    share = half // columns
+    tall = 2 * share
+
+    def signed(k):
+        return jnp.where(k < half, k, k - grid)
+
+    def opposite(k):
+        return jnp.where(k == 0, 0, grid - k)
+
+    def pick(lanes, at, values):
+        return jnp.sum(jnp.where(lanes == at, values, 0.0), 1, keepdims=True)
+
+    down = lax.broadcasted_iota(jnp.int32, (grid, grid), 0)
+    over = lax.broadcasted_iota(jnp.int32, (grid, grid), 1)
+    turned = pick(over, opposite(down), moduli[1:2, :])
+    factor_y = moduli[1:2, :]
+    mirror_y = jnp.sum(jnp.where(down == over, turned, 0.0), 0, keepdims=True)
+    lanes = over[:tall]
+    row = down[:tall]
+    upper = jnp.where(row >= share, 1, 0)
+    place = column * share + row - upper * share
+    kept = jnp.where((place & 1) == 0, place >> 1, half - (place >> 1))
+    kz = upper * half + jnp.where(place == 1, half // 2, kept)
+    factor_z = pick(lanes, kz, moduli[0:1, :])
+    mirror_z = pick(lanes, opposite(kz), moduli[0:1, :])
+    flat = signed(kz) * signed(kz) + signed(lanes) * signed(lanes)
+
+    def values(kx):
+        share_x = jnp.where((kx == 0) | (kx == half), 1.0, 2.0) * (0.5 * coulomb / grid**3)
+        factor_x = share_x * pick(over[:1], kx, moduli[2:3, :])
+        mirror_x = share_x * pick(over[:1], opposite(kx), moduli[2:3, :])
+        both = factor_x * factor_z * factor_y + mirror_x * mirror_z * mirror_y
+        radius = flat + signed(kx) * signed(kx)
+        squared = radius.astype(jnp.float32) * (1.0 / (grid * grid))
+        safe = jnp.where(radius > 0, squared, 1.0)
+        return jnp.where(radius > 0, both * jnp.exp(-screening[0] * squared) / safe, 0.0)
+
+    plain = values(slab * waves)
+    ends = values(half)
+    green[:tall, :] = jnp.where(slab == 0, 0.5 * (plain + ends), plain)
+    green[waves * tall :, :] = jnp.where(slab == 0, 0.5 * (plain - ends), 0.0)
+
+    @pl.loop(1, waves)
+    def _(w):
+        green[pl.ds(pl.multiple_of(w * tall, tall), tall), :] = values(slab * waves + w)
 
 
 def halves(table):
@@ -425,12 +466,11 @@
     kx = np.repeat(np.arange(slabs * waves), 2)
     px = np.tile(part, slabs * waves)
     table_x = turns(grid, kx[:, None], x[None, :], px[:, None])
-    top, rest = halves(table_x)
-    forward_x = np.stack([top, rest])
-    top, rest = halves(table_x.T)
-    pad = round_up(3 * top.shape[1], LANES) - 3 * top.shape[1]
-    inverse_x = np.concatenate([top, rest, top, np.zeros((grid, pad), top.dtype)], 1)
-    kz = np.broadcast_to(np.arange(half).reshape(columns, 1, share), (columns, 2, share)).reshape(-1)
+    table_x[1] = np.where(x % 2, -1.0, 1.0)
+    forward_x = np.concatenate(halves(table_x))
+    inverse_x = np.concatenate(halves(table_x.T))
+    kept = kept_waves(half, columns)
+    kz = np.broadcast_to(kept[:, None, :], (columns, 2, share)).reshape(-1)
     pk = np.broadcast_to(part.reshape(1, 2, 1), (columns, 2, share)).reshape(-1)
     zh = np.broadcast_to(np.arange(half).reshape(slabs, 1, pairs), (slabs, 2, pairs)).reshape(-1)
     pz = np.broadcast_to(part.reshape(1, 2, 1), (slabs, 2, pairs)).reshape(-1)
@@ -441,12 +481,12 @@
     pf = np.repeat(part, grid)
     table_y = turns(grid, ky[:, None], ky[None, :], pf[None, :] - pf[:, None])
     forward_y = np.stack(halves(table_y))
-    angle = 2.0 * np.pi * np.arange(half)[:, None] / grid
+    angle = 2.0 * np.pi * kept.reshape(-1, 1) / grid
     upper = np.arange(LANES)[None, :] >= LANES // 2
     twist = np.stack(
         [np.where(upper, np.cos(angle), 1.0), np.where(upper, np.sin(angle), 0.0)]
     ).astype(np.float32)
-    return forward_x, inverse_x, forward_z, inverse_z, forward_y, twist
+    return forward_x, inverse_x, forward_z, inverse_z, forward_y, twist, partners(half, columns)
 
 
 def chunks_of(waves, count):
@@ -456,9 +496,9 @@
 
 def solve_kernel(
     slabs, columns, waves, planes, rows, grid, chunks,
-    tile, green, table_fx, table_ix, table_fz, table_iz, table_y, twist, out,
-    rim_z, rim_y, rim_c, block, fx, fz, iz, fy, iy,
-    x_out, z_in, z_out, y_in, y_out, z_back, z_send, x_in, potential, y_left, y_right,
+    tile, moduli, screening, table_fx, table_ix, table_fz, table_iz, table_y, twist, moves, out,
+    green, rim_z, rim_y, rim_c,
+    x_out, z_in, z_out, y_in, y_out, z_back, z_send, x_in, y_top, y_rest, y_right,
     rim_send, rim_recv, gz_send, gz_recv, gy_send, gy_recv, by_send, by_recv, bz_send, bz_recv,
 ):
     half = grid // 2
@@ -503,42 +543,37 @@
     for copy in rims:
         copy.start()
 
-    for source, target in ((table_fx, fx), (table_fz, fz), (table_iz, iz)):
-        size = source.shape[2]
-        target[:, :size] = source[0]
-        target[:, size : 2 * size] = source[1]
-        target[:, 2 * size :] = source[0]
-    size = 2 * grid
-    fy[:size, :] = table_y[0]
-    fy[size : 2 * size, :] = table_y[0]
-    fy[2 * size :, :] = table_y[1]
-    iy[:, :size] = table_y[0]
-    iy[:, size : 2 * size] = table_y[0]
-    iy[:, 2 * size :] = table_y[1]
-    potential[planes + 3 :] = jnp.zeros_like(potential[planes + 3 :])
-
-    for copy in rims:
-        copy.wait()
-
-    def add_rims(at):
-        block[pl.ds(at * 4, 4)] = tile[pl.ds(at * 4, 4), :rows, :]
-        block[pl.ds(at * 4, 4), :8, :] += rim_y[pl.ds(at * 4, 4)]
-
-    pl.loop(0, planes // 4)(add_rims)
-    rim_z[:, :8, :] += rim_c[...]
-    block[:3] += rim_z[...]
-
-    def along_x(at):
-        top, rest = split(block[pl.ds(at * 4, 4)].reshape(4 * rows, grid))
-        values = lax.dot_general(
-            fx[...], jnp.concatenate([top, top, rest], 1), (((1,), (1,)), ((), ())),
-            preferred_element_type=jnp.float32,
-        )
+    out[planes + 3 :] = jnp.zeros_like(out[planes + 3 :])
+    across = (((1,), (1,)), ((), ()))
+
+    def product(left, right, form=(((1,), (0,)), ((), ()))):
+        return lax.dot_general(left, right, form, preferred_element_type=jnp.float32)
+
+    def along_x(at, rim):
+        value = tile[pl.ds(at * 4, 4), :rows, :]
+        head = value[:, :8] + rim_y[pl.ds(at * 4, 4)]
+        value = jnp.concatenate([head, value[:, 8:]], 1)
+        if rim is not None:
+            value = value + jnp.concatenate([rim, jnp.zeros((1, rows, grid), jnp.float32)], 0)
+        top, rest = split(value.reshape(4 * rows, grid))
+        both = product(table_fx[...], top, across)
+        values = both[:bins] + both[bins:] + product(table_fx[:bins, :], rest, across)
         for side in range(2):
             where = pl.ds(2 * at + side, bins, stride=pairs)
             x_out[where, :] = values[:, side * LANES : (side + 1) * LANES]
 
-    pl.loop(0, planes // 4)(along_x)
+    rims[1].wait()
+
+    @pl.loop(0, (planes // 4 - 2) // 2)
+    def _(turn_at):
+        along_x(2 * turn_at + 1, None)
+        along_x(2 * turn_at + 2, None)
+
+    rims[0].wait()
+    rims[2].wait()
+    rim_z[:, :8, :] += rim_c[...]
+    along_x(planes // 4 - 1, None)
+    along_x(0, rim_z[...])
 
     def gz_copy(q, step):
         w, n = chunks[q]
@@ -569,15 +604,17 @@
             gz_copy(q, step).start()
     z_in[slab] = x_out[pl.ds(pl.multiple_of(slab * waves * wide, wide), waves * wide), :]
 
+    fill_green(green, moduli, screening, slab, column, waves, columns)
     left = lax.broadcasted_iota(jnp.int32, (half, LANES), 1) < LANES // 2
     side = left[:share]
 
     def turn(value):
         return pltpu.roll(value, LANES // 2, 1)
 
-    def three(value):
+    def along_z(table, value):
         top, rest = split(value)
-        return jnp.concatenate([top, top, rest], 0)
+        both = product(table[0], jnp.concatenate([top, rest], 1))
+        return both[:, :LANES] + both[:, LANES:] + product(table[1], top)
 
     def to_z(q):
         for step in range(1, slabs):
@@ -587,7 +624,7 @@
         @pl.loop(first, first + count)
         def _(w):
             value = z_in[:, pl.ds(pl.multiple_of(w * wide, wide), wide), :].reshape(grid, LANES)
-            value = jnp.dot(fz[...], three(value), preferred_element_type=jnp.float32)
+            value = along_z(table_fz, value)
             value = value.reshape(columns, 2, share, LANES)
             re = value[:, 0].reshape(half, LANES)
             im = value[:, 1].reshape(half, LANES)
@@ -606,7 +643,6 @@
         for step in range(1, columns):
             gy_copy(q, step).wait_recv()
         first, count = chunks[q]
-        size = 2 * grid
 
         @pl.loop(0, count)
         def _(w):
@@ -619,18 +655,29 @@
                         to = pl.ds(pl.multiple_of(w * tall + h * share, share), share)
                         at = (p * columns + c) * rows
                         top, rest = split(pair[h])
-                        y_left[to, at : at + LANES] = top
-                        y_left[to, size + at : size + at + LANES] = rest
-                        y_left[to, 2 * size + at : 2 * size + at + LANES] = top
-
-        value = jnp.dot(y_left[: count * tall, :], fy[...], preferred_element_type=jnp.float32)
+                        y_top[to, at : at + LANES] = top
+                        y_rest[to, at : at + LANES] = rest
+
+        main_rows = size = count * tall
+        if first == 0:
+            size += tall
+            for target in (y_top, y_rest):
+                value = product(moves[column], target[:tall, :])
+                value = jnp.concatenate([value[:, :grid], -value[:, grid:]], 1)
+                target[main_rows:size, :] = value.astype(jnp.bfloat16)
+        top = y_top[:size, :]
+        both = product(jnp.concatenate([top, y_rest[:size, :]], 0), table_y[0])
+        value = both[:size] + both[size:] + product(top, table_y[1])
         factor = green[first * tall : (first + count) * tall, :]
+        if first == 0:
+            factor = jnp.concatenate([factor, green[waves * tall :, :]], 0)
         value = jnp.concatenate([value[:, :grid] * factor, value[:, grid:] * factor], 1)
+        if first == 0:
+            value = jnp.concatenate([value[:tall] + value[main_rows:], value[tall:main_rows]], 0)
+        size = main_rows
         top, rest = split(value)
-        y_right[: count * tall, :] = lax.dot_general(
-            jnp.concatenate([top, rest, top], 1), iy[...], (((1,), (1,)), ((), ())),
-            preferred_element_type=jnp.float32,
-        )
+        both = product(jnp.concatenate([top, rest], 0), table_y[0], across)
+        y_right[:size, :] = both[:size] + both[size:] + product(top, table_y[1], across)
 
         @pl.loop(0, count)
         def _(w):
@@ -669,7 +716,7 @@
             value = jnp.concatenate(
                 [v[c] for c in range(columns) for v in (re, im)], 0
             )
-            value = jnp.dot(iz[...], three(value), preferred_element_type=jnp.float32)
+            value = along_z(table_iz, value)
             where = pl.ds(pl.multiple_of(w * wide, wide), wide)
             z_send[:, where, :] = value.reshape(slabs, wide, LANES)
 
@@ -687,38 +734,41 @@
         for step in range(1, slabs):
             bz_copy(q, step).wait_recv()
 
-    spare = table_ix.shape[1] - 3 * bins
-
     def back_x(at):
         value = jnp.concatenate(
             [x_in[pl.ds(2 * at + s, bins, stride=pairs), :] for s in range(2)], 1
         )
         top, rest = split(value)
-        stack = [top, top, rest]
-        if spare:
-            stack.append(jnp.zeros((spare, 2 * LANES), jnp.bfloat16))
-        value = jnp.dot(
-            table_ix[...], jnp.concatenate(stack, 0), preferred_element_type=jnp.float32
+        both = product(table_ix[...], top)
+        value = both[:grid] + both[grid:] + product(table_ix[:grid, :], rest)
+        out[pl.ds(at * 4, 4), :rows, :] = value.T.reshape(4, rows, grid)
+
+    def rim_back(at):
+        planes_of = pl.ds(8 * at, 8)
+        return remote(
+            out.at[planes_of, pl.ds(0, 8)], out.at[planes_of, edge],
+            rim_send, rim_recv, 5 + at, (slab, beside(-1)),
         )
-        potential[pl.ds(at * 4, 4), :rows, :] = value.T.reshape(4, rows, grid)
-
-    pl.loop(0, planes // 4)(back_x)
-    rims_back = [
+
+    rims_back = [rim_back(at) for at in range(planes // 8)] + [
         remote(
-            potential.at[pl.ds(0, 3), main], potential.at[over_z, main],
+            out.at[pl.ds(0, 3), main], out.at[over_z, main],
             rim_send, rim_recv, 3, (around(-1), column),
         ),
         remote(
-            potential.at[body_z, pl.ds(0, 8)], potential.at[body_z, edge],
-            rim_send, rim_recv, 4, (slab, beside(-1)),
-        ),
-        remote(
-            potential.at[pl.ds(0, 3), pl.ds(0, 8)], potential.at[over_z, edge],
-            rim_send, rim_recv, 5, (around(-1), beside(-1)),
+            out.at[pl.ds(0, 3), pl.ds(0, 8)], out.at[over_z, edge],
+            rim_send, rim_recv, 4, (around(-1), beside(-1)),
         ),
     ]
-    for copy in rims_back:
-        copy.start()
+    for at in range(planes // 8):
+        back_x(2 * at)
+        back_x(2 * at + 1)
+        if at == 1:
+            for copy in rims_back[-2:]:
+                copy.start()
+        if at > 0:
+            rims_back[at - 1].start()
+    rims_back[planes // 8 - 1].start()
     for q in range(len(chunks)):
         for copy, steps in (
             (gz_copy, slabs), (gy_copy, columns), (by_copy, columns), (bz_copy, slabs)
@@ -728,19 +778,13 @@
     for copy in rims_back:
         copy.wait()
 
-    def give(at):
-        out[pl.ds(at * 4, 4)] = potential[pl.ds(at * 4, 4)]
-
-    pl.loop(0, out.shape[0] // 4)(give)
-
-
-def solve_fused(tile, green, slabs, columns, planes, rows, waves):
+
+def solve_fused(tile, moduli, screening, slabs, columns, planes, rows, waves):
     span_planes, span_rows, grid = tile.shape
     tables = solve_tables(grid, slabs, columns, waves, planes)
     chunks = chunks_of(waves, CHUNKS)
     most = max(n for _, n in chunks)
     wide, tall = planes, 2 * (grid // 2 // columns)
-    bins = 2 * slabs * waves
 
     def scratch(*shape):
         return pltpu.VMEM(shape, jnp.float32)
@@ -756,20 +800,18 @@
             solve_kernel, slabs, columns, waves, planes, rows, grid, chunks
         ),
         out_shape=jax.ShapeDtypeStruct(tile.shape, jnp.float32),
-        in_specs=[vmem()] * 8,
+        in_specs=[vmem()] * 2 + [smem()] + [vmem()] * 7,
         out_specs=vmem(),
         scratch_shapes=[
+            scratch((waves + 1) * tall, grid),
             scratch(3, rows, grid), scratch(planes, 8, grid), scratch(3, 8, grid),
-            scratch(planes, rows, grid),
-            narrow(bins, 3 * grid), narrow(grid, 3 * grid), narrow(grid, 3 * grid),
-            narrow(6 * grid, 2 * grid), narrow(2 * grid, 6 * grid),
             scratch(slabs * waves * wide, LANES), scratch(slabs, waves * wide, LANES),
             scratch(columns, waves * tall, LANES), scratch(columns, waves * tall, LANES),
             scratch(columns, waves * tall, LANES), scratch(columns, waves * tall, LANES),
             scratch(slabs, waves * wide, LANES), scratch(slabs * waves * wide, LANES),
-            scratch(*tile.shape),
-            narrow(most * tall, 6 * grid), scratch(most * tall, 2 * grid),
-            pltpu.SemaphoreType.DMA((6,)), pltpu.SemaphoreType.DMA((6,)),
+            narrow((most + 1) * tall, 2 * grid), narrow((most + 1) * tall, 2 * grid),
+            scratch(most * tall, 2 * grid),
+            *[pltpu.SemaphoreType.DMA((5 + planes // 8,))] * 2,
             *flags(slabs), *flags(columns), *flags(columns), *flags(slabs),
         ],
         compiler_params=pltpu.CompilerParams(
@@ -779,7 +821,7 @@
             flops=10**10, bytes_accessed=span_planes * span_rows * grid * 8, transcendentals=0
         ),
         name="solve",
-    )(tile, green, *(jnp.asarray(t) for t in tables))
+    )(tile, moduli, screening, *(jnp.asarray(t) for t in tables))
 
 
 def solve_tile(volume, kernel, tables, planes, rows, waves, slabs, columns):
@@ -828,14 +870,13 @@
     for cell in (cell_z, cell_y):
         high = jnp.max(jnp.where(alive, cell, 0), 1)
         bounds += [jnp.min(jnp.where(alive, cell, high[:, None]), 1), high]
-    bounds = jnp.stack(bounds)
     atoms = [v[None, :] for v in (key, *values)]
     sizes = (span_planes, span_rows, grid)
     count = live_atoms[None]
     tile = spread_atoms(count, bounds, atoms, bits, *sizes).reshape(sizes)
     if fast_sizes(slabs, columns, planes, rows, grid):
-        green = green_rows(moduli, screening, slab, column, grid, waves, columns)
-        padded = solve_fused(tile, green, slabs, columns, planes, rows, waves)
+        packed_waves = grid // 2 // slabs
+        padded = solve_fused(tile, moduli, screening, slabs, columns, planes, rows, packed_waves)
     else:
         tables = wave_tables(grid, slabs, columns, waves)
         kernel = influence(moduli, screening, slab, column, grid, waves, grid // columns)

time: 205 us -> 193 us (0.941); the launches traced: 202 us -> 193 us
  Pallas kernels: 165 us -> 159 us
  other arithmetic: 28.3 us -> 26 us
    pallas_call x1, Pallas kernels: 127 us -> 119 us  [solve_fused(): pl.pallas_call(functools.partial(solve_kernel, slabs, columns, waves, pla...]
where the time goes in v1:
time: 193 us
  Pallas kernels  159 us (82%)
  other arithmetic  26 us (13%)
  waiting for transfers between devices  3.74 us (2%)
  between operations  2.65 us (1%)
    pallas_call x1, Pallas kernels, solve_fused(): pl.pallas_call(functools.partial(solve_kernel, slabs, columns, waves, pla...  119 us
    pallas_call x1, Pallas kernels, interpolate_atoms(): pl.pallas_call(functools.partial(interpolate_kernel, rows, grid, bits), o...  22.9 us
    pallas_call x1, Pallas kernels, spread_atoms(): pl.pallas_call(functools.partial(spread_kernel, rows, grid, bits), out_sh...  16.9 us
    sort x1, other arithmetic, body(): lax.sort((key, slot, charge, fractions[0], fractions[1], fractions[2]), n...  13 us
    sort x1, other arithmetic, body(): lax.sort((slot, *(f[0] for f in forces)), num_keys=1, is_stable=False)  8.48 us
  transfers between devices with their start and end apart: 1, of which 1 were waited for; matrix products, arithmetic and copies ran while one was open for 0% of the time, Pallas kernels for 0%

profile of v1, /device:TPU:26, one launch (start us, length us, event | category | flops | bytes accessed | tf_op | source)
XLA Modules:
  0.0 193.1 jit_solution(8297799059497521902)
XLA Ops:
  0.0 1.3 shift-left_or_fusion
  1.3 1.3 fusion.3
  2.6 1.4 fusion.1
  4.6 13.0 %sort.66 = (s32[12288]{0:T(1024)S(1)}, s32[12288]{0:T(1024)S(1)}, f32[12288]{0:T(1024)}, f32[12288]{0:T(1024)}, f32[12288]{0:T(1024)}, /*index=5*/f32[12288]{0:T(1024)}) sort(s32[12288]{0:T(1024)S(1)} %fusion, s32[12288]{0:T(1024)S(1)} %iota.14, f32[12288]{0:T(1024)} %param.14, f32[12288]{0:T(1024)S(1)} %bitcast.23, f32[12288]{0:T(1024)S(1)} %bitcast.24, ...), dimensions={0}, to_apply=%region_2.3 | sort | flops 172032 | bytes 589824 | tf_op jit(solution)/shard_map/sort | solution.py:862
  17.6 0.0 copy-start
  18.3 0.1 select_reduce_fusion.1
  18.5 0.0 copy-start.1
  18.5 0.0 copy-start.2
  18.5 0.7 select_reduce_fusion
  19.2 0.0 copy-done
  19.2 0.0 copy-done.1
  19.2 0.0 copy-done.2
  19.2 16.9 %spread.1 = f32[3024,256]{1,0:T(8,128)} custom-call(s32[1]{0:T(128)} %bitcast.6.count, s32[48]{0:T(128)} %get-tuple-element.30.low_z, s32[48]{0:T(128)} %copy-done.2, s32[48]{0:T(128)} %get-tuple-element.29.low_y, s32[48]{0:T(128)} %copy-done.1, s32[1,12288]{1,0:T(1,128)} %bitcast.26, f32[1,12288]{1,0:T(1,128)} %bitcast.37, f32[1,12288]{1,0:T(1,128)} %bitcast.39, ...), custom_call_target="tpu_custom_call" | custom-call | flops 9512681472 | bytes 3096576 | tf_op jit(solution)/shard_map/spread/pallas_call | solution.py:249
  36.1 119.3 %solve.1 = f32[42,72,256]{2,1,0:T(8,128)} custom-call(f32[42,72,256]{2,1,0:T(8,128)} %bitcast.46, f32[3,256]{1,0:T(4,128)} %moduli.1, f32[1]{0:T(128)S(6)} %copy.16.screening, bf16[512,256]{1,0:T(8,128)(2,1)} %constant.15.clone.table_fx, bf16[512,256]{1,0:T(8,128)(2,1)} %constant.16.clone.table_ix, bf16[2,256,256]{2,1,0:T(8,128)(2,1)} %constant.17.clone.table_fz, ...), custom_call_target="tpu_custom_call" | custom-call | flops 10000000000 | bytes 6193152 | tf_op jit(solution)/shard_map/solve/pallas_call | solution.py:798
  155.4 22.9 %interpolate.1 = (f32[1,12288]{1,0:T(1,128)}, f32[1,12288]{1,0:T(1,128)}, f32[1,12288]{1,0:T(1,128)}) custom-call(s32[1]{0:T(128)} %bitcast.6.count, s32[48]{0:T(128)} %get-tuple-element.30.low_z, s32[48]{0:T(128)} %copy-done.2, s32[48]{0:T(128)} %get-tuple-element.29.low_y, s32[48]{0:T(128)} %copy-done.1, s32[1,12288]{1,0:T(1,128)} %bitcast.27, ...), custom_call_target="tpu_custom_call" | custom-call | flops 19025362944 | bytes 3096576 | tf_op jit(solution)/shard_map/interpolate/pallas_call | solution.py:270
  179.6 8.5 %sort.67 = (s32[12288]{0:T(1024)}, f32[12288]{0:T(1024)S(1)}, f32[12288]{0:T(1024)S(1)}, f32[12288]{0:T(1024)S(1)}) sort(s32[12288]{0:T(1024)S(1)} %get-tuple-element.17, f32[12288]{0:T(1024)} %bitcast.34, f32[12288]{0:T(1024)} %bitcast.35, f32[12288]{0:T(1024)} %bitcast.36), dimensions={0}, to_apply=%region_7.8 | sort | flops 172032 | bytes 393216 | tf_op jit(solution)/shard_map/sort | solution.py:886
  188.1 0.1 pad_maximum_fusion
  188.2 0.1 pad_dynamic-slice_fusion
  188.3 0.1 collective-permute-start
  188.4 3.7 %collective-permute-done = f32[3,4608]{1,0:T(4,128)S(1)} collective-permute-done((f32[3,4608]{1,0:T(4,128)S(1)}, f32[3,4608]{1,0:T(4,128)S(1)}, u32[]{:S(2)}, u32[]{:S(2)}) %collective-permute-start) | collective-permute-done | bytes 55328 | tf_op jit(solution)/shard_map/ppermute | solution.py:27
  192.2 0.9 slice_add_fusion
  (10 shorter events, 0.2 us)
Async XLA Ops:
  17.6 1.6 copy-start
  18.5 0.7 copy-start.1
  18.5 0.7 copy-start.2
  188.3 3.8 %collective-permute-start = (f32[3,4608]{1,0:T(4,128)S(1)}, f32[3,4608]{1,0:T(4,128)S(1)}, u32[]{:S(2)}, u32[]{:S(2)}) collective-permute-start(f32[3,4608]{1,0:T(4,128)S(1)} %pad_dynamic-slice_fusion), channel_id=1, source_target_pairs={{0,1},{1,2},{2,3},{3,0},{4,5},{5,6},{6,7},{7,4},{8,9},{9,10},{10,1... | collective-permute-start | bytes 165896 | tf_op jit(solution)/shard_map/ppermute | solution.py:27
